TPU v7x, 256 devices: a whole 4x4x8 slice. The times are simulated.
256 devices in a mesh: layer: 128 (over y_lo, x, z, core), src: 2 (over y_hi).
Axes of the slice: x: 4, y: 4 (y_hi: 2, y_lo: 2; y = y_hi * 2 + y_lo), z: 8, core: 2. Of those that a mesh axis runs over, the one named last changes fastest.
Arguments:
- down_maps: bfloat16 [128, 1664, 1664], P('layer'), may hold values from -1 to 1
- up_maps: bfloat16 [128, 1664, 1664], P('layer'), may hold values from -1 to 1
- local_traces: bfloat16 [128, 1664], P('src'), may hold values from -6 to 6
- src_depth: int32 [128], P('src'), may hold values from 0 to 127
Outputs:
- traces: bfloat16 [128, 128, 1664], P('layer', 'src')
- residual: bfloat16 [128, 128, 1664], P('layer', 'src')
All inputs are finite; a program needn't handle non-finite values.
Results may differ from a plain program's by a relative error of at most 0.035.
Values may be sent and summed in bfloat16 or wider, within the bound.
No kernel may reach another device: no remote copies, remote signals or barrier semaphores. Data moves between devices by JAX's collectives and lax.ppermute only.
A program may use at most 64 MiB of HBM per device.

v0:
```python
import jax
import jax.numpy as jnp
from jax import lax
from jax.experimental import pallas as pl
from jax.experimental.pallas import tpu as pltpu
from jax.sharding import PartitionSpec as P

BF = jnp.bfloat16
F32 = jnp.float32
EARLY = 1
SINGLES = 8
PAIRS = 24
VMEM = pl.BlockSpec(memory_space=pltpu.VMEM)
SMEM = pl.BlockSpec(memory_space=pltpu.SMEM)
HBM = pl.BlockSpec(memory_space=pltpu.HBM)


def limit(mib):
    return pltpu.CompilerParams(vmem_limit_bytes=mib * 2**20)


def dot(a, b):
    return jnp.dot(a, b, preferred_element_type=F32)


def by_block(extent, block, body):
    whole = extent // block

    def step(i, carry):
        body(pl.multiple_of(i * block, block), block)
        return carry

    if whole > 1:
        lax.fori_loop(0, whole, step, 0)
    else:
        body(0, block)
    if extent % block:
        body(whole * block, extent % block)


def cuts(width):
    step = -(-width // 2 // 256) * 256
    return [(0, step), (step, width)]


def through(x, parts):
    width = x.shape[1]
    spans = cuts(width)
    total = parts[-1][spans[-1][1] - spans[-1][0] :, :].astype(F32)
    for (low, high), part in zip(spans, parts):
        total = total + dot(x[:, low:high], part[0 : high - low, :])
    return total


def pick(meta, on_zero, on_one, name, after=None):
    first = () if after is None else (after,)

    def kernel(meta_ref, zero_ref, one_ref, *refs):
        out_ref = refs[len(first)]

        @pl.when(meta_ref[2] == 0)
        def _():
            pltpu.sync_copy(zero_ref, out_ref)

        @pl.when(meta_ref[2] != 0)
        def _():
            pltpu.sync_copy(one_ref, out_ref)

    return pl.pallas_call(
        kernel,
        out_shape=pltpu.VMEM(on_zero.shape, BF),
        in_specs=[SMEM, HBM, HBM] + [pl.BlockSpec(memory_space=pl.ANY)] * len(first),
        out_specs=VMEM,
        compiler_params=limit(8),
        name=name,
    )(meta, on_zero, on_one, *first)


def chip_product(meta, least, index, maps1, add1, maps2, add2):
    rows, width = add1.shape
    low, high = cuts(width)[index]
    last = high == width

    size = high - low + (rows if last else 0)
    block = 256 if not last else size // 4

    def kernel(meta_ref, maps1_ref, add1_ref, maps2_ref, add2_ref, out_ref, left_ref):
        @pl.when(meta_ref[0] >= least)
        def _():
            if last:
                left_ref[0 : high - low, :] = maps1_ref[low:high, :]
                left_ref[high - low :, :] = add1_ref[...]

            def body(start, count):
                left = left_ref[pl.ds(start, count), :] if last else maps1_ref[pl.ds(low + start, count), :]
                out_ref[pl.ds(start, count), :] = dot(left, maps2_ref[...]).astype(BF)

            by_block(size, block, body)
            if last:
                state = out_ref[high - low :, :].astype(F32) + add2_ref[...].astype(F32)
                out_ref[high - low :, :] = state.astype(BF)

    return pl.pallas_call(
        kernel,
        out_shape=jax.ShapeDtypeStruct((size, width), BF),
        in_specs=[SMEM] + [VMEM] * 4,
        out_specs=VMEM,
        scratch_shapes=[pltpu.VMEM((size if last else 16, width), BF)],
        compiler_params=limit(18),
        name="chip_product",
    )(meta, maps1, add1, maps2, add2)


def joint_product(meta, least, index, left, parts, name):
    width = left.shape[1]
    low, high = cuts(width)[index]
    last = high == width
    size = left.shape[0]
    block = 256 if not last else size // 4

    def kernel(meta_ref, left_ref, *refs):
        out_ref = refs[-1]
        part_refs = refs[:-1]

        def times(x):
            total = None
            for (a, b), part in zip(cuts(width), part_refs):
                piece = dot(x[:, a:b], part[0 : b - a, :])
                total = piece if total is None else total + piece
            return total

        @pl.when(meta_ref[0] >= least)
        def _():
            def body(start, count):
                out_ref[pl.ds(start, count), :] = times(left_ref[pl.ds(start, count), :]).astype(BF)

            by_block(size, block, body)
            if last:
                own = part_refs[-1][high - low :, :].astype(F32)
                out_ref[high - low :, :] = (out_ref[high - low :, :].astype(F32) + own).astype(BF)

    return pl.pallas_call(
        kernel,
        out_shape=jax.ShapeDtypeStruct(left.shape, BF),
        in_specs=[SMEM] + [VMEM] * (1 + len(parts)),
        out_specs=VMEM,
        compiler_params=limit(12),
        name=name,
    )(meta, left, *parts)


def begin(meta, maps2, add1, add2):
    def kernel(meta_ref, maps2_ref, add1_ref, add2_ref, out_ref):
        @pl.when(meta_ref[0] == 0)
        def _():
            value = add1_ref[...]

            def body(start, count):
                cols = pl.ds(start, count)
                out_ref[:, cols] = (dot(value, maps2_ref[:, cols]) + add2_ref[:, cols].astype(F32)).astype(BF)

            by_block(maps2_ref.shape[1], 512, body)

        @pl.when(meta_ref[0] != 0)
        def _():
            out_ref[...] = jnp.zeros(out_ref.shape, BF)

    return pl.pallas_call(
        kernel,
        out_shape=jax.ShapeDtypeStruct(add1.shape, BF),
        in_specs=[SMEM] + [VMEM] * 3,
        out_specs=VMEM,
        compiler_params=limit(8),
        name="begin",
    )(meta, maps2, add1, add2)


def advance(meta, position, arrived, maps, kept, out, block):
    def kernel(meta_ref, x_ref, kept_in, out_in, *refs):
        map_refs, (kept_ref, out_ref) = refs[:-2], refs[-2:]

        @pl.when(meta_ref[0] == position)
        def _():
            x = x_ref[...]
            kept_ref[...] = x
            width = x.shape[1]

            def body(start, count):
                cols = pl.ds(start, count)
                out_ref[:, cols] = through(x, [ref.at[:, cols] for ref in map_refs]).astype(BF)

            by_block(width, block, body)

        @pl.when(meta_ref[0] != position)
        def _():
            kept_ref[...] = kept_in[...]
            out_ref[...] = out_in[...]

    operands = list(maps)
    shape = jax.ShapeDtypeStruct(out.shape, BF)
    return pl.pallas_call(
        kernel,
        out_shape=(shape, shape),
        in_specs=[SMEM] + [VMEM] * (3 + len(operands)),
        out_specs=(VMEM, VMEM),
        compiler_params=limit(12),
        name="advance",
    )(meta, arrived, kept, out, *operands)


def late(maps, after, name):
    def kernel(maps_ref, after_ref, out_ref):
        pltpu.sync_copy(maps_ref, out_ref)

    return pl.pallas_call(
        kernel,
        out_shape=jax.ShapeDtypeStruct(maps.shape, BF),
        in_specs=[pl.BlockSpec(memory_space=pl.ANY)] * 2,
        out_specs=pl.BlockSpec(memory_space=pl.ANY),
        compiler_params=limit(8),
        name=name,
    )(maps, after)


def relay(meta, entering, parts):
    def kernel(meta_ref, x_ref, *refs):
        @pl.when((meta_ref[1] == 2) & (meta_ref[0] >= PAIRS))
        def _():
            refs[-1][...] = through(x_ref[...], refs[:-1]).astype(BF)

    return pl.pallas_call(
        kernel,
        out_shape=jax.ShapeDtypeStruct(entering.shape, BF),
        in_specs=[SMEM] + [VMEM] * (1 + len(parts)),
        out_specs=VMEM,
        compiler_params=limit(8),
        name="relay",
    )(meta, entering, *parts)


def two_layers(x, maps1_ref, maps2_ref, add1_ref, add2_ref, first_ref, second_ref):
    def layer(value, maps_ref, add_ref, out_ref):
        def body(start, count):
            cols = pl.ds(start, count)
            out_ref[:, cols] = dot(value, maps_ref[:, cols]) + add_ref[:, cols].astype(F32)

        by_block(maps_ref.shape[1], 512, body)

    layer(x, maps1_ref, add1_ref, first_ref)
    layer(first_ref[...].astype(BF), maps2_ref, add2_ref, second_ref)


def settle_most(meta, chips, kept, near, far, final, maps1, maps2, add1, add2, before1, before2):
    rows, width = kept.shape
    count = len(before1)

    def kernel(meta_ref, kept_ref, near_ref, far_ref, final_ref, m1, m2, a1, a2, *refs):
        part1, part2 = refs[:count], refs[count : 2 * count]
        first_ref, second_ref, x_ref = refs[2 * count :]
        position = meta_ref[0]
        role = meta_ref[1]
        from_near = role == 1

        def enter(parts):
            x = x_ref[...]

            def body(start, count):
                cols = pl.ds(start, count)
                x_ref[:, cols] = through(x, [ref.at[:, cols] for ref in parts]).astype(BF)

            by_block(width, 512, body)

        from_far = (role == 2) & (position >= PAIRS)
        from_final = position == chips - 1

        @pl.when(from_near)
        def _():
            x_ref[...] = near_ref[...]

        @pl.when(from_far)
        def _():
            x_ref[...] = far_ref[...]

        @pl.when(from_final)
        def _():
            x_ref[...] = final_ref[...]

        @pl.when(jnp.logical_not(from_near | from_far | from_final))
        def _():
            x_ref[...] = kept_ref[...]

        @pl.when(role == 4)
        def _():
            enter(part2)

        @pl.when((role == 2) | (role == 4))
        def _():
            enter(part1)

        @pl.when(role != 3)
        def _():
            two_layers(x_ref[...], m1, m2, a1, a2, first_ref, second_ref)

    shape = jax.ShapeDtypeStruct((rows, width), F32)
    return pl.pallas_call(
        kernel,
        out_shape=(shape, shape),
        in_specs=[SMEM] + [VMEM] * (8 + 2 * count),
        out_specs=(VMEM, VMEM),
        scratch_shapes=[pltpu.VMEM((rows, width), BF)],
        compiler_params=limit(16),
        name="settle_most",
    )(meta, kept, near, far, final, maps1, maps2, add1, add2, *before1, *before2)


def settle_third(meta, entering, maps1, maps2, add1, add2, first, second):
    rows, width = entering.shape

    def kernel(meta_ref, x_ref, m1, m2, a1, a2, first_in, second_in, first_ref, second_ref):
        @pl.when(meta_ref[1] == 3)
        def _():
            two_layers(x_ref[...], m1, m2, a1, a2, first_ref, second_ref)

        @pl.when(meta_ref[1] != 3)
        def _():
            first_ref[...] = first_in[...]
            second_ref[...] = second_in[...]

    shape = jax.ShapeDtypeStruct((rows, width), F32)
    return pl.pallas_call(
        kernel,
        out_shape=(shape, shape),
        in_specs=[SMEM] + [VMEM] * 7,
        out_specs=(VMEM, VMEM),
        compiler_params=limit(16),
        name="settle_third",
    )(meta, entering, maps1, maps2, add1, add2, first, second)


def finish(combined, own_add, partner, outer, maps_partner, maps_outer):
    def kernel(c_ref, a_ref, x_ref, o_ref, m1, m2, out_ref):
        part = dot(x_ref[...], m1[...]) + dot(o_ref[...], m2[...])
        out_ref[...] = (a_ref[...].astype(F32) - c_ref[...] + part).astype(BF)

    return pl.pallas_call(
        kernel,
        out_shape=jax.ShapeDtypeStruct(combined.shape, BF),
        in_specs=[VMEM] * 6,
        out_specs=VMEM,
        compiler_params=limit(16),
        name="finish",
    )(combined, own_add, partner, outer, maps_partner, maps_outer)


def shards(down_maps, up_maps, local_traces, src_depth):
    down, up = down_maps[0], up_maps[0]
    rows, width = local_traces.shape
    count = lax.axis_size("layer")
    chips = count // 2
    layer = lax.axis_index("layer")
    core = layer % 2
    chip = layer // 2
    position = jnp.where(core == 1, chip, chips - 1 - chip)
    role = jnp.where(
        position < SINGLES,
        0,
        jnp.where(position < PAIRS, 1 + (position - SINGLES) % 2, 1 + (position - PAIRS) % 4),
    )
    meta = jnp.stack([position, role, core]).astype(jnp.int32)

    def device(at):
        return (2 * at + 1, 2 * (chips - 1 - at))

    def links(steps):
        return [pair for a, b in steps for pair in zip(device(a), device(b))]

    def move(value, steps):
        return lax.ppermute(value, "layer", links(steps))

    partners = [(i, i ^ 1) for i in range(count)]
    zero = jnp.zeros((), BF)
    add2 = jnp.where((src_depth == layer)[:, None], local_traces, zero)
    add1 = jnp.where((src_depth == layer + 1 - 2 * core)[:, None], local_traces, zero)

    down = pltpu.with_memory_space_constraint(down, pltpu.HBM)
    up = pltpu.with_memory_space_constraint(up, pltpu.HBM)
    given = pick(meta, down, up, "pick_given")
    maps2 = pick(meta, up, down, "pick_own")
    maps1 = lax.ppermute(given, "layer", partners)
    thirds = range(len(cuts(width)))
    one = [chip_product(meta, EARLY, i, maps1, add1, maps2, add2) for i in thirds]
    pairs = [(e, e + 1) for e in range(SINGLES, chips, 2)]
    before1 = [move(part, pairs) for part in one]
    two = [joint_product(meta, SINGLES, i, before1[i], one, "pair_product") for i in thirds]
    quads = range(PAIRS, chips, 4)
    before2 = [move(part, [(e + 1, e + 3) for e in quads]) for part in two]
    four = [joint_product(meta, PAIRS, i, before2[i], two, "quad_product") for i in thirds]

    stops = [(at, one) for at in range(EARLY, SINGLES)]
    stops += [(e + 1, two) for e in range(SINGLES, PAIRS, 2)]
    stops += [(e + 3, four) for e in range(PAIRS, chips - 4, 4)]
    kept = jnp.zeros((rows, width), BF)
    out = begin(meta, maps2, add1, add2)
    last = 0
    for at, maps in stops:
        arrived = move(out, [(last, at)])
        if at == stops[-2][0]:
            ahead = out
        kept, out = advance(meta, at, arrived, maps, kept, out, width if maps is four else 512)
        last = at

    far = move(out, [(e - 1, e + 1) for e in quads])
    final = move(out, [(last, chips - 1)])
    near = move(out, [(e - 1, e) for e in list(range(SINGLES, PAIRS, 2)) + list(quads)])
    maps1 = late(maps1, ahead, "late_first")
    given = pick(meta, down, up, "late_given", ahead)
    passed = move(relay(meta, far, two), [(e + 1, e + 2) for e in quads])
    first, second = settle_most(
        meta, chips, kept, near, far, final, maps1, maps2, add1, add2, before1, before2
    )
    first, second = settle_third(meta, passed, maps1, maps2, add1, add2, first, second)

    combined = second + lax.ppermute(first, "layer", partners) - add2.astype(F32)
    rounded = combined.astype(BF)
    partner = lax.ppermute(rounded, "layer", partners)
    outward = [(i, i + 1) for i in range(1, count - 1, 2)]
    outer = lax.ppermute(rounded, "layer", outward + [(b, a) for a, b in outward])
    residual = finish(combined, add2, partner, outer, maps2, given)
    return (rounded[None], residual[None])


def solution(mesh):
    placed = (P("layer", None, None), P("layer", None, None), P("src", None), P("src"))
    return jax.shard_map(
        shards,
        mesh=mesh,
        in_specs=placed,
        out_specs=(P("layer", "src", None), P("layer", "src", None)),
        check_vma=False,
    )
```

profile of v0, /device:TPU:1, one launch (start us, length us, event | category | flops | bytes accessed | tf_op | source)
XLA Modules:
  0.0 307.2 jit_solution(14361386337288302788)
XLA Ops:
  0.8 5.5 %pick_given.1 = bf16[1664,1664]{1,0:T(8,128)(2,1)} custom-call(s32[3]{0:T(128)S(1)} %pad_add_fusion.meta_ref, bf16[1664,1664]{1,0:T(8,128)(2,1)} %bitcast.12, bf16[1664,1664]{1,0:T(8,128)(2,1)} %bitcast.9), custom_call_target="tpu_custom_call" | custom-call | tf_op jit(solution)/shard_map/pick_given/pallas_call | solution.py:69
  6.3 3.2 %collective-permute-start.1 = (bf16[1664,1664]{1,0:T(8,128)(2,1)}, bf16[1664,1664]{1,0:T(8,128)(2,1)}, u32[]{:S(2)}, u32[]{:S(2)}) collective-permute-start(bf16[1664,1664]{1,0:T(8,128)(2,1)} %pick_given.1), channel_id=1, source_target_pairs={{0,2},{2,0},{4,6},{6,4},{8,10},{10,8},{12,14},{14,12},{16,18},{18,... | collective-permute-start | bytes 16613384 | tf_op jit(solution)/shard_map/ppermute | solution.py:389
  9.5 3.1 %pick_own.1.maps2_ref.m2.m1 = bf16[1664,1664]{1,0:T(8,128)(2,1)S(1)} custom-call(s32[3]{0:T(128)S(1)} %pad_add_fusion.meta_ref, bf16[1664,1664]{1,0:T(8,128)(2,1)} %bitcast.10, bf16[1664,1664]{1,0:T(8,128)(2,1)} %bitcast.13), custom_call_target="tpu_custom_call" | custom-call | tf_op jit(solution)/shard_map/pick_own/pallas_call | solution.py:69
  12.6 2.4 copy-done
  15.2 3.4 %collective-permute-done.1.maps1_ref.maps_ref = bf16[1664,1664]{1,0:T(8,128)(2,1)} collective-permute-done((bf16[1664,1664]{1,0:T(8,128)(2,1)}, bf16[1664,1664]{1,0:T(8,128)(2,1)}, u32[]{:S(2)}, u32[]{:S(2)}) %collective-permute-start.1) | collective-permute-done | bytes 5537824 | tf_op jit(solution)/shard_map/ppermute | solution.py:389
  18.5 2.6 copy-done.1
  21.1 2.6 chip_product.2.refs_0_
  23.7 0.9 collective-permute-start.9
  24.6 2.6 chip_product.3.refs_1_
  27.2 0.8 collective-permute-start.10
  28.0 2.1 begin.1.out_in
  30.1 13.2 %collective-permute-start = (bf16[64,1664]{1,0:T(8,128)(2,1)S(1)}, bf16[64,1664]{1,0:T(8,128)(2,1)S(1)}, u32[]{:S(2)}, u32[]{:S(2)}) collective-permute-start(bf16[64,1664]{1,0:T(8,128)(2,1)S(1)} %begin.1.out_in), channel_id=1, source_target_pairs={{2,6},{252,248},{3,7},{253,249}} | collective-permute-start | bytes 638984 | tf_op jit(solution)/shard_map/ppermute | solution.py:378
  43.9 0.9 collective-permute-start.19
  44.8 1.3 collective-permute-done.x_ref
  46.7 0.7 collective-permute-start.2
  48.0 0.7 collective-permute-start.3
  49.3 0.7 collective-permute-start.4
  49.9 0.6 advance.27
  50.5 0.7 collective-permute-start.5
  51.2 0.6 advance.28
  51.8 0.7 collective-permute-start.6
  53.1 0.8 collective-permute-start.20
  54.5 0.7 collective-permute-start.7
  55.8 0.7 collective-permute-start.8
  56.5 0.6 advance.31
  57.1 0.9 collective-permute-start.11
  58.5 0.7 collective-permute-start.12
  59.2 0.6 advance.33
  59.8 0.7 collective-permute-start.13
  60.5 0.6 advance.34
  61.1 0.7 collective-permute-start.14
  61.8 0.6 advance.35
  62.4 0.7 collective-permute-start.15
  63.1 0.6 advance.36
  63.7 0.7 collective-permute-start.16
  65.0 0.7 collective-permute-start.17
  66.2 0.7 collective-permute-start.18
  68.1 0.6 advance.39
  68.7 0.7 collective-permute-start.21
  69.4 0.6 advance.40
  69.9 0.7 collective-permute-start.22
  70.6 0.6 advance.41
  71.2 0.7 collective-permute-start.23
  72.5 0.7 collective-permute-start.24
  73.8 0.7 collective-permute-start.25
  74.5 0.6 advance.44
  75.1 0.7 collective-permute-start.26
  75.8 0.6 advance.45
  76.4 0.7 collective-permute-start.27
  77.7 0.7 collective-permute-start.28
  78.3 0.8 advance.47
  79.2 0.7 collective-permute-start.29
  79.8 0.7 collective-permute-start.31
  80.5 0.7 collective-permute-start.32
  81.8 0.8 collective-permute-start.30
  82.6 2.8 late_first.1.m1
  85.5 3.5 %settle_most.1 = (f32[64,1664]{1,0:T(8,128)S(1)}, f32[64,1664]{1,0:T(8,128)S(1)}) custom-call(s32[3]{0:T(128)S(1)} %pad_add_fusion.meta_ref, bf16[64,1664]{1,0:T(8,128)(2,1)S(1)} %get-tuple-element.101.kept_ref, bf16[64,1664]{1,0:T(8,128)(2,1)S(1)} %collective-permute-done.31.near_ref, bf16[64,1664]{1,0:T(8,128)(2,1)S(1)} %collective-permute-done.29.x_ref.far_ref, ...), custom_call_target="tpu_custom_call" | custom-call | tf_op jit(solution)/shard_map/settle_most/pallas_call | solution.py:305
  89.0 0.6 settle_third.1
  89.6 206.0 %collective-permute-start.33 = (f32[64,1664]{1,0:T(8,128)S(1)}, f32[64,1664]{1,0:T(8,128)S(1)}, u32[]{:S(2)}, u32[]{:S(2)}) collective-permute-start(f32[64,1664]{1,0:T(8,128)S(1)} %get-tuple-element.105), channel_id=1, source_target_pairs={{0,2},{2,0},{4,6},{6,4},{8,10},{10,8},{12,14},{14,12},{16,18},{18,... | collective-permute-start | bytes 1277960 | tf_op jit(solution)/shard_map/ppermute | solution.py:423
  295.7 1.4 collective-permute-done.33
  297.6 3.3 %collective-permute-start.35 = (bf16[64,1664]{1,0:T(8,128)(2,1)S(1)}, bf16[64,1664]{1,0:T(8,128)(2,1)S(1)}, u32[]{:S(2)}, u32[]{:S(2)}) collective-permute-start(bf16[64,1664]{1,0:T(8,128)(2,1)S(1)} %get-tuple-element.106), channel_id=1, source_target_pairs={{2,4},{6,8},{10,12},{14,16},{18,20},{22,24},{26,28},{30,32},{34,36... | collective-permute-start | bytes 638984 | tf_op jit(solution)/shard_map/ppermute | solution.py:427
  301.0 3.1 %late_given.1.m2 = bf16[1664,1664]{1,0:T(8,128)(2,1)S(1)} custom-call(s32[3]{0:T(128)S(1)} %pad_add_fusion.meta_ref, bf16[1664,1664]{1,0:T(8,128)(2,1)} %bitcast.14, bf16[1664,1664]{1,0:T(8,128)(2,1)} %bitcast.11, bf16[64,1664]{1,0:T(8,128)(2,1)S(1)} %get-tuple-element.96.out_in.after_ref.refs_0_), custom_call_target="tpu_custom_call" | custom-call | tf_op jit(solution)/shard_map/late_given/pallas_call | solution.py:69
  304.1 0.7 collective-permute-done.35.o_ref
  304.8 2.4 finish.1
  (67 shorter events, 10.0 us)
Async XLA Ops:
  6.3 12.2 %collective-permute-start.1 = (bf16[1664,1664]{1,0:T(8,128)(2,1)}, bf16[1664,1664]{1,0:T(8,128)(2,1)}, u32[]{:S(2)}, u32[]{:S(2)}) collective-permute-start(bf16[1664,1664]{1,0:T(8,128)(2,1)} %pick_given.1), channel_id=1, source_target_pairs={{0,2},{2,0},{4,6},{6,4},{8,10},{10,8},{12,14},{14,12},{16,18},{18,... | collective-permute-start | bytes 16613384 | tf_op jit(solution)/shard_map/ppermute | solution.py:389
  9.5 5.6 %copy-start.4 = (s32[64]{0:T(128)S(1)}, s32[64]{0:T(128)}, u32[]{:S(2)}) copy-start(s32[64]{0:T(128)} %param.7) | copy-start | bytes 772
  9.5 5.6 %copy-start.2 = (bf16[64,1664]{1,0:T(8,128)(2,1)S(1)}, bf16[64,1664]{1,0:T(8,128)(2,1)}, u32[]{:S(2)}) copy-start(bf16[64,1664]{1,0:T(8,128)(2,1)} %param.6) | copy-start | bytes 638980
  12.6 2.4 copy-start
  18.5 2.6 copy-start.1
  23.7 19.6 %collective-permute-start.9 = (bf16[1024,1664]{1,0:T(8,128)(2,1)S(1)}, bf16[1024,1664]{1,0:T(8,128)(2,1)S(1)}, u32[]{:S(2)}, u32[]{:S(2)}) collective-permute-start(bf16[1024,1664]{1,0:T(8,128)(2,1)S(1)} %chip_product.2.refs_0_), channel_id=1, source_target_pairs={{34,38},{220,216},{42,46},{212,208},{50,54},{204,200},{58,62},{196... | collective-permute-start | bytes 10223624 | tf_op jit(solution)/shard_map/ppermute | solution.py:378
  27.2 25.3 %collective-permute-start.10 = (bf16[704,1664]{1,0:T(8,128)(2,1)S(1)}, bf16[704,1664]{1,0:T(8,128)(2,1)S(1)}, u32[]{:S(2)}, u32[]{:S(2)}) collective-permute-start(bf16[704,1664]{1,0:T(8,128)(2,1)S(1)} %chip_product.3.refs_1_), channel_id=1, source_target_pairs={{34,38},{220,216},{42,46},{212,208},{50,54},{204,200},{58,62},{196... | collective-permute-start | bytes 7028744 | tf_op jit(solution)/shard_map/ppermute | solution.py:378
  30.1 16.0 %collective-permute-start = (bf16[64,1664]{1,0:T(8,128)(2,1)S(1)}, bf16[64,1664]{1,0:T(8,128)(2,1)S(1)}, u32[]{:S(2)}, u32[]{:S(2)}) collective-permute-start(bf16[64,1664]{1,0:T(8,128)(2,1)S(1)} %begin.1.out_in), channel_id=1, source_target_pairs={{2,6},{252,248},{3,7},{253,249}} | collective-permute-start | bytes 638984 | tf_op jit(solution)/shard_map/ppermute | solution.py:378
  43.9 23.6 %collective-permute-start.19 = (bf16[1024,1664]{1,0:T(8,128)(2,1)S(1)}, bf16[1024,1664]{1,0:T(8,128)(2,1)S(1)}, u32[]{:S(2)}, u32[]{:S(2)}) collective-permute-start(bf16[1024,1664]{1,0:T(8,128)(2,1)S(1)} %pair_product.2.refs_0_), channel_id=1, source_target_pairs={{102,110},{152,144},{118,126},{136,128},{134,142},{120,112},{150,1... | collective-permute-start | bytes 10223624 | tf_op jit(solution)/shard_map/ppermute | solution.py:378
  46.7 0.7 collective-permute-start.2
  48.0 0.7 collective-permute-start.3
  49.3 0.7 collective-permute-start.4
  50.5 0.7 collective-permute-start.5
  51.8 2.1 collective-permute-start.6
  53.1 13.8 %collective-permute-start.20 = (bf16[704,1664]{1,0:T(8,128)(2,1)S(1)}, bf16[704,1664]{1,0:T(8,128)(2,1)S(1)}, u32[]{:S(2)}, u32[]{:S(2)}) collective-permute-start(bf16[704,1664]{1,0:T(8,128)(2,1)S(1)} %pair_product.3.refs_1_), channel_id=1, source_target_pairs={{102,110},{152,144},{118,126},{136,128},{134,142},{120,112},{150,1... | collective-permute-start | bytes 7028744 | tf_op jit(solution)/shard_map/ppermute | solution.py:378
  54.5 0.7 collective-permute-start.7
  55.8 0.7 collective-permute-start.8
  57.1 0.9 collective-permute-start.11
  58.5 0.7 collective-permute-start.12
  59.8 0.7 collective-permute-start.13
  61.1 0.7 collective-permute-start.14
  62.4 0.7 collective-permute-start.15
  63.7 0.7 collective-permute-start.16
  65.0 0.7 collective-permute-start.17
  66.2 1.8 collective-permute-start.18
  68.7 0.7 collective-permute-start.21
  69.9 0.7 collective-permute-start.22
  71.2 0.7 collective-permute-start.23
  72.5 0.7 collective-permute-start.24
  73.8 0.7 collective-permute-start.25
  75.1 0.7 collective-permute-start.26
  76.4 0.7 collective-permute-start.27
  77.7 0.7 collective-permute-start.28
  79.2 2.0 collective-permute-start.29
  79.8 5.6 %collective-permute-start.31 = (bf16[64,1664]{1,0:T(8,128)(2,1)S(1)}, bf16[64,1664]{1,0:T(8,128)(2,1)S(1)}, u32[]{:S(2)}, u32[]{:S(2)}) collective-permute-start(bf16[64,1664]{1,0:T(8,128)(2,1)S(1)} %get-tuple-element.100), channel_id=1, source_target_pairs={{30,34},{224,220},{38,42},{216,212},{46,50},{208,204},{54,58},{200... | collective-permute-start | bytes 638984 | tf_op jit(solution)/shard_map/ppermute | solution.py:378
  80.5 4.9 %collective-permute-start.32 = (bf16[64,1664]{1,0:T(8,128)(2,1)S(1)}, bf16[64,1664]{1,0:T(8,128)(2,1)S(1)}, u32[]{:S(2)}, u32[]{:S(2)}) collective-permute-start(bf16[64,1664]{1,0:T(8,128)(2,1)S(1)} %get-tuple-element.100), channel_id=1, source_target_pairs={{238,254},{16,0},{239,255},{17,1}} | collective-permute-start | bytes 638984 | tf_op jit(solution)/shard_map/ppermute | solution.py:378
  81.2 4.2 %slice-start = ((s8[5537792]{0:T(1024)(128)(4,1)}), s8[4194304]{0:T(1024)(128)(4,1)S(1)}, s32[]{:S(2)}) async-start(s8[5537792]{0:T(1024)(128)(4,1)} %bitcast.7), calls=%async_computation | async-start | bytes 8388608
  81.8 3.7 %slice-start.1 = ((s8[5537792]{0:T(1024)(128)(4,1)}), s8[1343488]{0:T(1024)(128)(4,1)S(1)}, s32[]{:S(2)}) async-start(s8[5537792]{0:T(1024)(128)(4,1)} %bitcast.7), calls=%async_computation.1 | async-start | bytes 2686976
  81.8 7.2 %collective-permute-start.30 = (bf16[64,1664]{1,0:T(8,128)(2,1)S(1)}, bf16[64,1664]{1,0:T(8,128)(2,1)S(1)}, u32[]{:S(2)}, u32[]{:S(2)}) collective-permute-start(bf16[64,1664]{1,0:T(8,128)(2,1)S(1)} %relay.1), channel_id=1, source_target_pairs={{102,106},{152,148},{118,122},{136,132},{134,138},{120,116},{150,1... | collective-permute-start | bytes 638984 | tf_op jit(solution)/shard_map/ppermute | solution.py:378
  89.6 207.4 %collective-permute-start.33 = (f32[64,1664]{1,0:T(8,128)S(1)}, f32[64,1664]{1,0:T(8,128)S(1)}, u32[]{:S(2)}, u32[]{:S(2)}) collective-permute-start(f32[64,1664]{1,0:T(8,128)S(1)} %get-tuple-element.105), channel_id=1, source_target_pairs={{0,2},{2,0},{4,6},{6,4},{8,10},{10,8},{12,14},{14,12},{16,18},{18,... | collective-permute-start | bytes 1277960 | tf_op jit(solution)/shard_map/ppermute | solution.py:423
  297.2 7.0 %copy-start.3 = (bf16[64,1664]{1,0:T(8,128)(2,1)}, bf16[64,1664]{1,0:T(8,128)(2,1)S(1)}, u32[]{:S(2)}) copy-start(bf16[64,1664]{1,0:T(8,128)(2,1)S(1)} %get-tuple-element.106) | copy-start | bytes 638980
  297.2 6.9 %collective-permute-start.34 = (bf16[64,1664]{1,0:T(8,128)(2,1)S(1)}, bf16[64,1664]{1,0:T(8,128)(2,1)S(1)}, u32[]{:S(2)}, u32[]{:S(2)}) collective-permute-start(bf16[64,1664]{1,0:T(8,128)(2,1)S(1)} %get-tuple-element.106), channel_id=1, source_target_pairs={{0,2},{2,0},{4,6},{6,4},{8,10},{10,8},{12,14},{14,12},{16,18},{18,... | collective-permute-start | bytes 638984 | tf_op jit(solution)/shard_map/ppermute | solution.py:425
  297.6 7.2 %collective-permute-start.35 = (bf16[64,1664]{1,0:T(8,128)(2,1)S(1)}, bf16[64,1664]{1,0:T(8,128)(2,1)S(1)}, u32[]{:S(2)}, u32[]{:S(2)}) collective-permute-start(bf16[64,1664]{1,0:T(8,128)(2,1)S(1)} %get-tuple-element.106), channel_id=1, source_target_pairs={{2,4},{6,8},{10,12},{14,16},{18,20},{22,24},{26,28},{30,32},{34,36... | collective-permute-start | bytes 638984 | tf_op jit(solution)/shard_map/ppermute | solution.py:427
where the time goes:
time: 308 us; the launch traced here: 307 us
  starting transfers between devices  248 us (81%)
  Pallas kernels  45.4 us (15%)
  waiting for transfers between devices  6.81 us (2%)
  local copies, waits for them, and re-layouts  5.03 us (2%)
    ppermute x1, starting transfers between devices, shards(): lax.ppermute(first, 'layer', partners)  206 us
    ppermute x32, starting transfers between devices, move(): return lax.ppermute(value, 'layer', links(steps))  35.1 us
    pallas_call x24, Pallas kernels, advance(): pl.pallas_call(kernel, out_shape=(shape, shape), in_specs=[SMEM] + [VMEM]...  14.2 us
    pallas_call x3, Pallas kernels, pick(): pl.pallas_call(kernel, out_shape=pltpu.VMEM(on_zero.shape, BF), in_specs=...  11.8 us
  transfers between devices with their start and end apart: 36, of which 4 were waited for; matrix products, arithmetic and copies ran while one was open for 0% of the time, Pallas kernels for 9%

commit v1 on v0

--- a/solution.py
+++ b/solution.py
@@ -8,7 +8,7 @@
 BF = jnp.bfloat16
 F32 = jnp.float32
 EARLY = 1
-SINGLES = 8
+SINGLES = 6
 PAIRS = 24
 VMEM = pl.BlockSpec(memory_space=pltpu.VMEM)
 SMEM = pl.BlockSpec(memory_space=pltpu.SMEM)

time: 308 us -> 310 us (level)
    ppermute x32 -> x31, starting transfers between devices: 35.1 us -> 34.5 us  [move(): return lax.ppermute(value, 'layer', links(steps))]
    pallas_call x24 -> x23, Pallas kernels: 14.2 us -> 13.6 us  [advance(): pl.pallas_call(kernel, out_shape=(shape, shape), in_specs=[SMEM] + [VMEM]...]
  transfers between devices with their start and end apart: 36 -> 35, of which waited for: 4 -> 4; matrix products, arithmetic and copies ran while one was open for 0% -> 0% of each run, Pallas kernels for 9% -> 9%
where the time goes in v1:
time: 310 us
  starting transfers between devices  250 us (81%)
  Pallas kernels  44.6 us (14%)
  waiting for transfers between devices  8.46 us (3%)
  local copies, waits for them, and re-layouts  4.98 us (2%)
    ppermute x1, starting transfers between devices, shards(): lax.ppermute(first, 'layer', partners)  209 us
    ppermute x31, starting transfers between devices, move(): return lax.ppermute(value, 'layer', links(steps))  34.5 us
    pallas_call x23, Pallas kernels, advance(): pl.pallas_call(kernel, out_shape=(shape, shape), in_specs=[SMEM] + [VMEM]...  13.6 us
    pallas_call x3, Pallas kernels, pick(): pl.pallas_call(kernel, out_shape=pltpu.VMEM(on_zero.shape, BF), in_specs=...  11.8 us
  transfers between devices with their start and end apart: 35, of which 4 were waited for; matrix products, arithmetic and copies ran while one was open for 0% of the time, Pallas kernels for 9%

profile of v1, /device:TPU:1, one launch (start us, length us, event | category | flops | bytes accessed | tf_op | source)
XLA Modules:
  0.0 309.7 jit_solution(8083053769871154741)
XLA Ops:
  0.8 5.5 %pick_given.1 = bf16[1664,1664]{1,0:T(8,128)(2,1)} custom-call(s32[3]{0:T(128)S(1)} %pad_add_fusion.meta_ref, bf16[1664,1664]{1,0:T(8,128)(2,1)} %bitcast.12, bf16[1664,1664]{1,0:T(8,128)(2,1)} %bitcast.9), custom_call_target="tpu_custom_call" | custom-call | tf_op jit(solution)/shard_map/pick_given/pallas_call | solution.py:69
  6.3 3.2 %collective-permute-start.1 = (bf16[1664,1664]{1,0:T(8,128)(2,1)}, bf16[1664,1664]{1,0:T(8,128)(2,1)}, u32[]{:S(2)}, u32[]{:S(2)}) collective-permute-start(bf16[1664,1664]{1,0:T(8,128)(2,1)} %pick_given.1), channel_id=1, source_target_pairs={{0,2},{2,0},{4,6},{6,4},{8,10},{10,8},{12,14},{14,12},{16,18},{18,... | collective-permute-start | bytes 16613384 | tf_op jit(solution)/shard_map/ppermute | solution.py:389
  9.5 3.1 %pick_own.1.maps2_ref.m2.m1 = bf16[1664,1664]{1,0:T(8,128)(2,1)S(1)} custom-call(s32[3]{0:T(128)S(1)} %pad_add_fusion.meta_ref, bf16[1664,1664]{1,0:T(8,128)(2,1)} %bitcast.10, bf16[1664,1664]{1,0:T(8,128)(2,1)} %bitcast.13), custom_call_target="tpu_custom_call" | custom-call | tf_op jit(solution)/shard_map/pick_own/pallas_call | solution.py:69
  12.6 2.4 copy-done
  15.1 3.4 %collective-permute-done.1.maps1_ref.maps_ref = bf16[1664,1664]{1,0:T(8,128)(2,1)} collective-permute-done((bf16[1664,1664]{1,0:T(8,128)(2,1)}, bf16[1664,1664]{1,0:T(8,128)(2,1)}, u32[]{:S(2)}, u32[]{:S(2)}) %collective-permute-start.1) | collective-permute-done | bytes 5537824 | tf_op jit(solution)/shard_map/ppermute | solution.py:389
  18.5 2.6 copy-done.1
  21.1 2.7 chip_product.2.refs_0_
  23.9 1.0 collective-permute-start.7
  24.9 2.6 chip_product.3.refs_1_
  27.5 0.8 collective-permute-start.8
  28.9 0.9 collective-permute-start.18
  29.8 2.1 begin.1.out_in
  31.8 13.2 %collective-permute-start = (bf16[64,1664]{1,0:T(8,128)(2,1)S(1)}, bf16[64,1664]{1,0:T(8,128)(2,1)S(1)}, u32[]{:S(2)}, u32[]{:S(2)}) collective-permute-start(bf16[64,1664]{1,0:T(8,128)(2,1)S(1)} %begin.1.out_in), channel_id=1, source_target_pairs={{2,6},{252,248},{3,7},{253,249}} | collective-permute-start | bytes 638984 | tf_op jit(solution)/shard_map/ppermute | solution.py:378
  45.1 2.8 collective-permute-done.x_ref
  47.9 0.6 advance.23
  48.5 0.7 collective-permute-start.2
  49.2 0.6 advance.24
  49.7 0.7 collective-permute-start.3
  50.4 0.6 advance.25
  51.0 0.7 collective-permute-start.4
  51.7 0.6 advance.26
  52.3 0.7 collective-permute-start.5
  53.6 0.8 collective-permute-start.19
  54.4 0.6 advance.27
  55.0 0.7 collective-permute-start.6
  56.3 0.7 collective-permute-start.9
  57.6 0.7 collective-permute-start.10
  58.3 0.8 advance.30
  59.0 0.7 collective-permute-start.11
  60.3 0.7 collective-permute-start.12
  61.6 0.7 collective-permute-start.13
  62.3 0.6 advance.33
  62.9 0.7 collective-permute-start.14
  63.6 0.6 advance.34
  64.2 0.7 collective-permute-start.15
  64.9 0.6 advance.35
  65.4 0.7 collective-permute-start.16
  66.7 0.7 collective-permute-start.17
  69.2 0.7 collective-permute-start.20
  69.8 0.6 advance.38
  70.4 0.7 collective-permute-start.21
  71.1 0.6 advance.39
  71.7 0.7 collective-permute-start.22
  72.4 0.6 advance.40
  73.0 0.7 collective-permute-start.23
  74.3 0.7 collective-permute-start.24
  75.6 0.7 collective-permute-start.25
  76.9 0.7 collective-permute-start.26
  77.6 0.6 advance.44
  78.1 0.7 collective-permute-start.27
  78.8 0.6 advance.45
  79.4 0.9 collective-permute-start.28
  80.3 0.7 collective-permute-start.30
  81.0 0.7 collective-permute-start.31
  82.3 0.7 collective-permute-start.29
  83.0 2.6 late_first.1.m1
  85.5 3.5 %settle_most.1 = (f32[64,1664]{1,0:T(8,128)S(1)}, f32[64,1664]{1,0:T(8,128)S(1)}) custom-call(s32[3]{0:T(128)S(1)} %pad_add_fusion.meta_ref, bf16[64,1664]{1,0:T(8,128)(2,1)S(1)} %get-tuple-element.97.kept_ref, bf16[64,1664]{1,0:T(8,128)(2,1)S(1)} %collective-permute-done.30.near_ref, bf16[64,1664]{1,0:T(8,128)(2,1)S(1)} %collective-permute-done.28.x_ref.far_ref, ...), custom_call_target="tpu_custom_call" | custom-call | tf_op jit(solution)/shard_map/settle_most/pallas_call | solution.py:305
  89.1 0.6 settle_third.1
  89.7 208.5 %collective-permute-start.32 = (f32[64,1664]{1,0:T(8,128)S(1)}, f32[64,1664]{1,0:T(8,128)S(1)}, u32[]{:S(2)}, u32[]{:S(2)}) collective-permute-start(f32[64,1664]{1,0:T(8,128)S(1)} %get-tuple-element.101), channel_id=1, source_target_pairs={{0,2},{2,0},{4,6},{6,4},{8,10},{10,8},{12,14},{14,12},{16,18},{18,... | collective-permute-start | bytes 1277960 | tf_op jit(solution)/shard_map/ppermute | solution.py:423
  298.2 1.4 collective-permute-done.32
  300.2 3.2 %collective-permute-start.34 = (bf16[64,1664]{1,0:T(8,128)(2,1)S(1)}, bf16[64,1664]{1,0:T(8,128)(2,1)S(1)}, u32[]{:S(2)}, u32[]{:S(2)}) collective-permute-start(bf16[64,1664]{1,0:T(8,128)(2,1)S(1)} %get-tuple-element.102), channel_id=1, source_target_pairs={{2,4},{6,8},{10,12},{14,16},{18,20},{22,24},{26,28},{30,32},{34,36... | collective-permute-start | bytes 638984 | tf_op jit(solution)/shard_map/ppermute | solution.py:427
  303.4 3.1 %late_given.1.m2 = bf16[1664,1664]{1,0:T(8,128)(2,1)S(1)} custom-call(s32[3]{0:T(128)S(1)} %pad_add_fusion.meta_ref, bf16[1664,1664]{1,0:T(8,128)(2,1)} %bitcast.14, bf16[1664,1664]{1,0:T(8,128)(2,1)} %bitcast.11, bf16[64,1664]{1,0:T(8,128)(2,1)S(1)} %get-tuple-element.92.out_in.after_ref.refs_0_), custom_call_target="tpu_custom_call" | custom-call | tf_op jit(solution)/shard_map/late_given/pallas_call | solution.py:69
  306.5 0.8 collective-permute-done.34.o_ref
  307.3 2.4 finish.1
  (64 shorter events, 8.9 us)
Async XLA Ops:
  6.3 12.2 %collective-permute-start.1 = (bf16[1664,1664]{1,0:T(8,128)(2,1)}, bf16[1664,1664]{1,0:T(8,128)(2,1)}, u32[]{:S(2)}, u32[]{:S(2)}) collective-permute-start(bf16[1664,1664]{1,0:T(8,128)(2,1)} %pick_given.1), channel_id=1, source_target_pairs={{0,2},{2,0},{4,6},{6,4},{8,10},{10,8},{12,14},{14,12},{16,18},{18,... | collective-permute-start | bytes 16613384 | tf_op jit(solution)/shard_map/ppermute | solution.py:389
  9.5 5.5 %copy-start.4 = (s32[64]{0:T(128)S(1)}, s32[64]{0:T(128)}, u32[]{:S(2)}) copy-start(s32[64]{0:T(128)} %param.7) | copy-start | bytes 772
  9.5 5.5 %copy-start.2 = (bf16[64,1664]{1,0:T(8,128)(2,1)S(1)}, bf16[64,1664]{1,0:T(8,128)(2,1)}, u32[]{:S(2)}) copy-start(bf16[64,1664]{1,0:T(8,128)(2,1)} %param.6) | copy-start | bytes 638980
  12.6 2.4 copy-start
  18.5 2.6 copy-start.1
  21.1 8.7 %slice-start = ((s8[5537792]{0:T(1024)(128)(4,1)}), s8[4194304]{0:T(1024)(128)(4,1)S(1)}, s32[]{:S(2)}) async-start(s8[5537792]{0:T(1024)(128)(4,1)} %bitcast.7), calls=%async_computation | async-start | bytes 8388608
  23.9 5.9 %slice-start.1 = ((s8[5537792]{0:T(1024)(128)(4,1)}), s8[1343488]{0:T(1024)(128)(4,1)S(1)}, s32[]{:S(2)}) async-start(s8[5537792]{0:T(1024)(128)(4,1)} %bitcast.7), calls=%async_computation.1 | async-start | bytes 2686976
  23.9 4.4 %collective-permute-start.7 = (bf16[1024,1664]{1,0:T(8,128)(2,1)S(1)}, bf16[1024,1664]{1,0:T(8,128)(2,1)S(1)}, u32[]{:S(2)}, u32[]{:S(2)}) collective-permute-start(bf16[1024,1664]{1,0:T(8,128)(2,1)S(1)} %chip_product.2.refs_0_), channel_id=1, source_target_pairs={{26,30},{228,224},{34,38},{220,216},{42,46},{212,208},{50,54},{204... | collective-permute-start | bytes 10223624 | tf_op jit(solution)/shard_map/ppermute | solution.py:378
  27.5 25.5 %collective-permute-start.8 = (bf16[704,1664]{1,0:T(8,128)(2,1)S(1)}, bf16[704,1664]{1,0:T(8,128)(2,1)S(1)}, u32[]{:S(2)}, u32[]{:S(2)}) collective-permute-start(bf16[704,1664]{1,0:T(8,128)(2,1)S(1)} %chip_product.3.refs_1_), channel_id=1, source_target_pairs={{26,30},{228,224},{34,38},{220,216},{42,46},{212,208},{50,54},{204... | collective-permute-start | bytes 7028744 | tf_op jit(solution)/shard_map/ppermute | solution.py:378
  28.9 39.1 %collective-permute-start.18 = (bf16[1024,1664]{1,0:T(8,128)(2,1)S(1)}, bf16[1024,1664]{1,0:T(8,128)(2,1)S(1)}, u32[]{:S(2)}, u32[]{:S(2)}) collective-permute-start(bf16[1024,1664]{1,0:T(8,128)(2,1)S(1)} %pair_product.2.refs_0_), channel_id=1, source_target_pairs={{102,110},{152,144},{118,126},{136,128},{134,142},{120,112},{150,1... | collective-permute-start | bytes 10223624 | tf_op jit(solution)/shard_map/ppermute | solution.py:378
  31.8 16.0 %collective-permute-start = (bf16[64,1664]{1,0:T(8,128)(2,1)S(1)}, bf16[64,1664]{1,0:T(8,128)(2,1)S(1)}, u32[]{:S(2)}, u32[]{:S(2)}) collective-permute-start(bf16[64,1664]{1,0:T(8,128)(2,1)S(1)} %begin.1.out_in), channel_id=1, source_target_pairs={{2,6},{252,248},{3,7},{253,249}} | collective-permute-start | bytes 638984 | tf_op jit(solution)/shard_map/ppermute | solution.py:378
  48.5 0.7 collective-permute-start.2
  49.7 0.7 collective-permute-start.3
  51.0 0.7 collective-permute-start.4
  52.3 2.1 collective-permute-start.5
  53.6 13.8 %collective-permute-start.19 = (bf16[704,1664]{1,0:T(8,128)(2,1)S(1)}, bf16[704,1664]{1,0:T(8,128)(2,1)S(1)}, u32[]{:S(2)}, u32[]{:S(2)}) collective-permute-start(bf16[704,1664]{1,0:T(8,128)(2,1)S(1)} %pair_product.3.refs_1_), channel_id=1, source_target_pairs={{102,110},{152,144},{118,126},{136,128},{134,142},{120,112},{150,1... | collective-permute-start | bytes 7028744 | tf_op jit(solution)/shard_map/ppermute | solution.py:378
  55.0 0.7 collective-permute-start.6
  56.3 0.7 collective-permute-start.9
  57.6 0.7 collective-permute-start.10
  59.0 0.7 collective-permute-start.11
  60.3 0.7 collective-permute-start.12
  61.6 0.7 collective-permute-start.13
  62.9 0.7 collective-permute-start.14
  64.2 0.7 collective-permute-start.15
  65.4 0.7 collective-permute-start.16
  66.7 1.8 collective-permute-start.17
  69.2 0.7 collective-permute-start.20
  70.4 0.7 collective-permute-start.21
  71.7 0.7 collective-permute-start.22
  73.0 0.7 collective-permute-start.23
  74.3 0.7 collective-permute-start.24
  75.6 0.7 collective-permute-start.25
  76.9 0.7 collective-permute-start.26
  78.1 0.7 collective-permute-start.27
  79.4 2.3 collective-permute-start.28
  80.3 5.2 %collective-permute-start.30 = (bf16[64,1664]{1,0:T(8,128)(2,1)S(1)}, bf16[64,1664]{1,0:T(8,128)(2,1)S(1)}, u32[]{:S(2)}, u32[]{:S(2)}) collective-permute-start(bf16[64,1664]{1,0:T(8,128)(2,1)S(1)} %get-tuple-element.96), channel_id=1, source_target_pairs={{22,26},{232,228},{30,34},{224,220},{38,42},{216,212},{46,50},{208... | collective-permute-start | bytes 638984 | tf_op jit(solution)/shard_map/ppermute | solution.py:378
  81.0 4.5 %collective-permute-start.31 = (bf16[64,1664]{1,0:T(8,128)(2,1)S(1)}, bf16[64,1664]{1,0:T(8,128)(2,1)S(1)}, u32[]{:S(2)}, u32[]{:S(2)}) collective-permute-start(bf16[64,1664]{1,0:T(8,128)(2,1)S(1)} %get-tuple-element.96), channel_id=1, source_target_pairs={{238,254},{16,0},{239,255},{17,1}} | collective-permute-start | bytes 638984 | tf_op jit(solution)/shard_map/ppermute | solution.py:378
  82.3 6.8 %collective-permute-start.29 = (bf16[64,1664]{1,0:T(8,128)(2,1)S(1)}, bf16[64,1664]{1,0:T(8,128)(2,1)S(1)}, u32[]{:S(2)}, u32[]{:S(2)}) collective-permute-start(bf16[64,1664]{1,0:T(8,128)(2,1)S(1)} %relay.1), channel_id=1, source_target_pairs={{102,106},{152,148},{118,122},{136,132},{134,138},{120,116},{150,1... | collective-permute-start | bytes 638984 | tf_op jit(solution)/shard_map/ppermute | solution.py:378
  89.7 209.9 %collective-permute-start.32 = (f32[64,1664]{1,0:T(8,128)S(1)}, f32[64,1664]{1,0:T(8,128)S(1)}, u32[]{:S(2)}, u32[]{:S(2)}) collective-permute-start(f32[64,1664]{1,0:T(8,128)S(1)} %get-tuple-element.101), channel_id=1, source_target_pairs={{0,2},{2,0},{4,6},{6,4},{8,10},{10,8},{12,14},{14,12},{16,18},{18,... | collective-permute-start | bytes 1277960 | tf_op jit(solution)/shard_map/ppermute | solution.py:423
  299.7 6.8 %copy-start.3 = (bf16[64,1664]{1,0:T(8,128)(2,1)}, bf16[64,1664]{1,0:T(8,128)(2,1)S(1)}, u32[]{:S(2)}) copy-start(bf16[64,1664]{1,0:T(8,128)(2,1)S(1)} %get-tuple-element.102) | copy-start | bytes 638980
  299.7 6.8 %collective-permute-start.33 = (bf16[64,1664]{1,0:T(8,128)(2,1)S(1)}, bf16[64,1664]{1,0:T(8,128)(2,1)S(1)}, u32[]{:S(2)}, u32[]{:S(2)}) collective-permute-start(bf16[64,1664]{1,0:T(8,128)(2,1)S(1)} %get-tuple-element.102), channel_id=1, source_target_pairs={{0,2},{2,0},{4,6},{6,4},{8,10},{10,8},{12,14},{14,12},{16,18},{18,... | collective-permute-start | bytes 638984 | tf_op jit(solution)/shard_map/ppermute | solution.py:425
  300.2 7.2 %collective-permute-start.34 = (bf16[64,1664]{1,0:T(8,128)(2,1)S(1)}, bf16[64,1664]{1,0:T(8,128)(2,1)S(1)}, u32[]{:S(2)}, u32[]{:S(2)}) collective-permute-start(bf16[64,1664]{1,0:T(8,128)(2,1)S(1)} %get-tuple-element.102), channel_id=1, source_target_pairs={{2,4},{6,8},{10,12},{14,16},{18,20},{22,24},{26,28},{30,32},{34,36... | collective-permute-start | bytes 638984 | tf_op jit(solution)/shard_map/ppermute | solution.py:427
